TPU v7x, 32 devices: a whole 2x2x4 slice. The times are simulated.
32 devices in a mesh: wide: 8 (over y, x, core), narrow: 4 (over z).
Axes of the slice: x: 2, y: 2, z: 4, core: 2. Of those that a mesh axis runs over, the one named last changes fastest.
Arguments:
- layer_input: bfloat16 [4, 2048, 2048], P(None, 'wide'), may hold values from -6 to 6
- grad_out: bfloat16 [4, 2048, 2048], P(None, 'wide'), may hold values from -6 to 6
- lengths: int32 [4, 8], replicated, may hold values from 1 to 1024, 2048 in all within a row
- w_query: bfloat16 [2048, 2048], P('wide', 'narrow'), may hold values from -0.125 to 0.125
- w_key: bfloat16 [2048, 1024], P('wide', 'narrow'), may hold values from -0.125 to 0.125
- w_value: bfloat16 [2048, 1024], P('wide', 'narrow'), may hold values from -0.125 to 0.125
- w_out: bfloat16 [2048, 2048], P('narrow', 'wide'), may hold values from -0.75 to 0.75
- w_gate: bfloat16 [2048, 6144], P('wide', 'narrow'), may hold values from -0.125 to 0.125
- w_up: bfloat16 [2048, 6144], P('wide', 'narrow'), may hold values from -0.125 to 0.125
- w_down: bfloat16 [6144, 2048], P('narrow', 'wide'), may hold values from -0.078125 to 0.078125
- gain_attn: float32 [2048], replicated, may hold values from 0.25 to 1.75
- gain_ffn: float32 [2048], replicated, may hold values from 0.25 to 1.75
- gain_query: float32 [128], replicated, may hold values from 0.25 to 1.75
- gain_key: float32 [128], replicated, may hold values from 0.25 to 1.75
Outputs:
- output: bfloat16 [4, 2048, 2048], P(None, 'wide')
- grad_input: float32 [4, 2048, 2048], P(None, 'wide')
- grad_wquery: float32 [2048, 2048], P('wide', 'narrow')
- grad_wkey: float32 [2048, 1024], P('wide', 'narrow')
- grad_wvalue: float32 [2048, 1024], P('wide', 'narrow')
- grad_wout: float32 [2048, 2048], P('narrow', 'wide')
- grad_wgate: float32 [2048, 6144], P('wide', 'narrow')
- grad_wup: float32 [2048, 6144], P('wide', 'narrow')
- grad_wdown: float32 [6144, 2048], P('narrow', 'wide')
- grad_gattn: float32 [2048], replicated
- grad_gffn: float32 [2048], replicated
- grad_gquery: float32 [128], replicated
- grad_gkey: float32 [128], replicated
Inputs may be any that keep to these rules, and one draw needn't show every extreme that they name: `lengths`: each row cuts the 2048 tokens of its micro-batch into 8 consecutive pieces in order; pieces 0 to 6 are documents and the last piece is padding. A row's pieces sum to 2048, and its largest piece is exactly 1024.
All inputs are finite; a program needn't handle non-finite values.
Results may differ from a plain program's by a relative error of at most 0.022.
Values may be sent and summed in bfloat16 or wider, within the bound.
A program may use at most 256 MiB of HBM per device.

v0:
```python
import math
import jax
import jax.numpy as jnp
from jax import lax
from jax.sharding import PartitionSpec as P

HD = 128
NDOC = 8
EPSILON = 1e-06
THETA = 1000000.0


def rms_norm(values, gain):
    return values * lax.rsqrt(jnp.mean(values * values, axis=-1, keepdims=True) + EPSILON) * gain


def unit_rows(values):
    return values * lax.rsqrt(jnp.mean(values * values, axis=-1, keepdims=True) + EPSILON)


def rotate(values, cosine, sine):
    midway = values.shape[-1] // 2
    turned = jnp.concatenate([-values[..., midway:], values[..., :midway]], axis=-1)
    return values * cosine + turned * sine


def layout(lengths_row, total):
    finish = jnp.cumsum(lengths_row)
    starts = finish - lengths_row
    places = jnp.arange(total, dtype=jnp.int32)
    segment = jnp.sum((places[:, None] >= finish[None, :]).astype(jnp.int32), axis=1)
    member = segment[:, None] == jnp.arange(finish.shape[0], dtype=jnp.int32)[None, :]
    opening = jnp.sum(jnp.where(member, starts[None, :], 0), axis=1)
    return (segment, places - opening)


def angles(place):
    frequency = jnp.exp(-math.log(THETA) * jnp.arange(0, HD, 2).astype(jnp.float32) / HD)
    turning = place.astype(jnp.float32)[:, None] * frequency[None, :]
    turning = jnp.concatenate([turning, turning], axis=-1)
    return (jnp.cos(turning), jnp.sin(turning))


def allowed(query_seg, query_idx, key_seg, key_idx):
    same_doc = query_seg[:, None] == key_seg[None, :]
    causal = key_idx[None, :] <= query_idx[:, None]
    usable = (key_seg[None, :] != NDOC - 1) | (key_idx[None, :] == query_idx[:, None])
    return same_doc & causal & usable


def attention_scores(query_low, key_all, mask_local, factor):
    scores = (
        jnp.einsum("tgrd,kgd->grtk", query_low, key_all, preferred_element_type=jnp.float32)
        * factor
    )
    return jnp.where(mask_local[None, None], scores, -1e30)


def one_batch(row_input, grad_row, lengths_row, gathered, gains):
    w_query, w_key, w_value, w_out, w_gate, w_up, w_down = gathered
    gain_attn, gain_ffn, gain_query, gain_key = gains
    tok_rows = row_input.shape[0]
    total = tok_rows * lax.axis_size("wide")
    groups = w_key.shape[1] // HD
    repeat = w_query.shape[1] // w_key.shape[1]
    factor = 1.0 / math.sqrt(HD)
    first_row = lax.axis_index("wide") * tok_rows
    segment, place = layout(lengths_row, total)
    positions = jnp.arange(total, dtype=jnp.int32)
    query_seg = lax.dynamic_slice_in_dim(segment, first_row, tok_rows)
    query_idx = lax.dynamic_slice_in_dim(positions, first_row, tok_rows)
    mask_local = allowed(query_seg, query_idx, segment, positions)
    cosine, sine = angles(lax.dynamic_slice_in_dim(place, first_row, tok_rows))

    def head_norm(rows, gain):
        return rotate(rms_norm(rows, gain), cosine[:, None, :], sine[:, None, :])

    input_float = row_input.astype(jnp.float32)
    grad_float = grad_row.astype(jnp.float32)
    normed_one, pull_one = jax.vjp(lambda rows: rms_norm(rows, gain_attn), input_float)
    hidden_one = normed_one.astype(jnp.bfloat16)
    query_raw = jnp.dot(hidden_one, w_query, preferred_element_type=jnp.float32).reshape(
        tok_rows, groups * repeat, HD
    )
    key_raw = jnp.dot(hidden_one, w_key, preferred_element_type=jnp.float32).reshape(
        tok_rows, groups, HD
    )
    value_low = jnp.dot(hidden_one, w_value, preferred_element_type=jnp.float32).astype(
        jnp.bfloat16
    )
    query_turned, pull_query = jax.vjp(head_norm, query_raw, gain_query)
    key_turned, pull_key = jax.vjp(head_norm, key_raw, gain_key)
    query_low = query_turned.astype(jnp.bfloat16).reshape(tok_rows, groups, repeat, HD)
    key_low = key_turned.astype(jnp.bfloat16).reshape(tok_rows, groups * HD)
    key_all, value_all = (
        lax.all_gather(key_low, "wide", axis=0, tiled=True),
        lax.all_gather(value_low, "wide", axis=0, tiled=True),
    )
    key_all = key_all.reshape(total, groups, HD)
    value_all = value_all.reshape(total, groups, HD)
    scores = attention_scores(query_low, key_all, mask_local, factor)
    highest = jnp.max(scores, axis=-1, keepdims=True)
    exponent = jnp.exp(scores - highest)
    denominator = jnp.sum(exponent, axis=-1, keepdims=True)
    log_total = highest + jnp.log(denominator)
    probs_low = (exponent / denominator).astype(jnp.bfloat16)
    mixed = jnp.einsum("grtk,kgd->tgrd", probs_low, value_all, preferred_element_type=jnp.float32)
    mixed_low = mixed.reshape(tok_rows, groups * repeat * HD).astype(jnp.bfloat16)
    attn_part = jnp.dot(mixed_low, w_out, preferred_element_type=jnp.float32)
    middle = input_float + lax.psum(attn_part.astype(jnp.bfloat16), "narrow").astype(jnp.float32)
    normed_two, pull_two = jax.vjp(lambda rows: rms_norm(rows, gain_ffn), middle)
    hidden_two = normed_two.astype(jnp.bfloat16)
    unit_two = unit_rows(middle)
    gate = jnp.dot(hidden_two, w_gate, preferred_element_type=jnp.float32)
    up_proj = jnp.dot(hidden_two, w_up, preferred_element_type=jnp.float32)
    active, pull_active = jax.vjp(
        lambda gate_in, up_in: jax.nn.silu(gate_in) * up_in, gate, up_proj
    )
    active_low = active.astype(jnp.bfloat16)
    ffn_part = jnp.dot(active_low, w_down, preferred_element_type=jnp.float32)
    output_low = (
        middle + lax.psum(ffn_part.astype(jnp.bfloat16), "narrow").astype(jnp.float32)
    ).astype(jnp.bfloat16)
    grad_wdown = jnp.einsum("tf,td->fd", active_low, grad_row, preferred_element_type=jnp.float32)
    grad_active = jnp.einsum("td,fd->tf", grad_row, w_down, preferred_element_type=jnp.float32)
    grad_gate, grad_upper = pull_active(grad_active)
    gate_back = grad_gate.astype(jnp.bfloat16)
    upper_back = grad_upper.astype(jnp.bfloat16)
    grad_wgate = jnp.einsum("td,tf->df", hidden_two, gate_back, preferred_element_type=jnp.float32)
    grad_wup = jnp.einsum("td,tf->df", hidden_two, upper_back, preferred_element_type=jnp.float32)
    partial_two = jnp.einsum(
        "tf,df->td", gate_back, w_gate, preferred_element_type=jnp.float32
    ) + jnp.einsum("tf,df->td", upper_back, w_up, preferred_element_type=jnp.float32)
    gain_two = jnp.sum(partial_two * unit_two, axis=0)
    grad_middle = (
        grad_float
        + pull_two(lax.psum(partial_two.astype(jnp.bfloat16), "narrow").astype(jnp.float32))[0]
    )
    middle_low = grad_middle.astype(jnp.bfloat16)
    grad_wout = jnp.einsum("th,td->hd", mixed_low, middle_low, preferred_element_type=jnp.float32)
    grad_mixed = jnp.einsum("td,hd->th", middle_low, w_out, preferred_element_type=jnp.float32)
    grad_mixed = grad_mixed.astype(jnp.bfloat16).reshape(tok_rows, groups, repeat, HD)
    scores = attention_scores(query_low, key_all, mask_local, factor)
    probs = jnp.exp(scores - log_total)
    grad_probs = jnp.einsum(
        "tgrd,kgd->grtk", grad_mixed, value_all, preferred_element_type=jnp.float32
    )
    weighted = jnp.sum(probs * grad_probs, axis=-1, keepdims=True)
    grad_scores = (probs * (grad_probs - weighted)).astype(jnp.bfloat16)
    grad_turned = (
        jnp.einsum("grtk,kgd->tgrd", grad_scores, key_all, preferred_element_type=jnp.float32)
        * factor
    )
    grad_keyall = (
        jnp.einsum("grtk,tgrd->kgd", grad_scores, query_low, preferred_element_type=jnp.float32)
        * factor
    )
    grad_valueall = jnp.einsum(
        "grtk,tgrd->kgd", probs.astype(jnp.bfloat16), grad_mixed, preferred_element_type=jnp.float32
    )
    grad_keys, grad_values = (
        lax.psum_scatter(
            grad_keyall.reshape(total, groups * HD).astype(jnp.bfloat16),
            "wide",
            scatter_dimension=0,
            tiled=True,
        ).astype(jnp.float32),
        lax.psum_scatter(
            grad_valueall.reshape(total, groups * HD).astype(jnp.bfloat16),
            "wide",
            scatter_dimension=0,
            tiled=True,
        ).astype(jnp.float32),
    )
    grad_qraw, gain_q = pull_query(grad_turned.reshape(tok_rows, groups * repeat, HD))
    grad_kraw, gain_k = pull_key(grad_keys.reshape(tok_rows, groups, HD))
    query_back = grad_qraw.reshape(tok_rows, groups * repeat * HD).astype(jnp.bfloat16)
    key_back = grad_kraw.reshape(tok_rows, groups * HD).astype(jnp.bfloat16)
    value_back = grad_values.astype(jnp.bfloat16)
    grad_wquery = jnp.einsum(
        "td,th->dh", hidden_one, query_back, preferred_element_type=jnp.float32
    )
    grad_wkey = jnp.einsum("td,th->dh", hidden_one, key_back, preferred_element_type=jnp.float32)
    grad_wvalue = jnp.einsum(
        "td,th->dh", hidden_one, value_back, preferred_element_type=jnp.float32
    )
    partial_one = (
        jnp.einsum("th,dh->td", query_back, w_query, preferred_element_type=jnp.float32)
        + jnp.einsum("th,dh->td", key_back, w_key, preferred_element_type=jnp.float32)
        + jnp.einsum("th,dh->td", value_back, w_value, preferred_element_type=jnp.float32)
    )
    gain_one = jnp.sum(partial_one * unit_rows(input_float), axis=0)
    grad_input = (
        grad_middle
        + pull_one(lax.psum(partial_one.astype(jnp.bfloat16), "narrow").astype(jnp.float32))[0]
    )
    weight_grads = (
        grad_wquery,
        grad_wkey,
        grad_wvalue,
        grad_wout,
        grad_wgate,
        grad_wup,
        grad_wdown,
    )
    return (output_low, grad_input, weight_grads, (gain_one, gain_two, gain_q, gain_k))


def local(
    layer_input,
    grad_out,
    lengths,
    w_query,
    w_key,
    w_value,
    w_out,
    w_gate,
    w_up,
    w_down,
    gain_attn,
    gain_ffn,
    gain_query,
    gain_key,
):
    width = lax.axis_size("wide")
    shards = (w_query, w_key, w_value, w_out, w_gate, w_up, w_down)
    along_rows = (True, True, True, False, True, True, False)
    gains = (gain_attn, gain_ffn, gain_query, gain_key)
    totals = tuple(
        (
            jnp.zeros(
                (
                    (piece.shape[0] * width, piece.shape[1])
                    if rows_first
                    else (piece.shape[0], piece.shape[1] * width)
                ),
                jnp.float32,
            )
            for piece, rows_first in zip(shards, along_rows)
        )
    )
    gain_terms = tuple((jnp.zeros(gain.shape, jnp.float32) for gain in gains))
    outputs = []
    grad_inputs = []
    for micro in range(layer_input.shape[0]):
        gathered = (
            lax.all_gather(w_query, "wide", axis=0, tiled=True),
            lax.all_gather(w_key, "wide", axis=0, tiled=True),
            lax.all_gather(w_value, "wide", axis=0, tiled=True),
            lax.all_gather(w_out, "wide", axis=1, tiled=True),
            lax.all_gather(w_gate, "wide", axis=0, tiled=True),
            lax.all_gather(w_up, "wide", axis=0, tiled=True),
            lax.all_gather(w_down, "wide", axis=1, tiled=True),
        )
        output, grad_input, weight_grads, gain_grads = one_batch(
            layer_input[micro], grad_out[micro], lengths[micro], gathered, gains
        )
        outputs.append(output)
        grad_inputs.append(grad_input)
        gain_terms = tuple((running + fresh for running, fresh in zip(gain_terms, gain_grads)))
        totals = tuple((running + fresh for running, fresh in zip(totals, weight_grads)))
    results = (
        lax.psum_scatter(
            totals[0].astype(jnp.bfloat16), "wide", scatter_dimension=0, tiled=True
        ).astype(jnp.float32),
        lax.psum_scatter(
            totals[1].astype(jnp.bfloat16), "wide", scatter_dimension=0, tiled=True
        ).astype(jnp.float32),
        lax.psum_scatter(
            totals[2].astype(jnp.bfloat16), "wide", scatter_dimension=0, tiled=True
        ).astype(jnp.float32),
        lax.psum_scatter(
            totals[3].astype(jnp.bfloat16), "wide", scatter_dimension=1, tiled=True
        ).astype(jnp.float32),
        lax.psum_scatter(
            totals[4].astype(jnp.bfloat16), "wide", scatter_dimension=0, tiled=True
        ).astype(jnp.float32),
        lax.psum_scatter(
            totals[5].astype(jnp.bfloat16), "wide", scatter_dimension=0, tiled=True
        ).astype(jnp.float32),
        lax.psum_scatter(
            totals[6].astype(jnp.bfloat16), "wide", scatter_dimension=1, tiled=True
        ).astype(jnp.float32),
    )
    gain_total = lax.psum(gain_terms, ("wide", "narrow"))
    return (
        jnp.stack(outputs),
        jnp.stack(grad_inputs),
        results[0],
        results[1],
        results[2],
        results[3],
        results[4],
        results[5],
        results[6],
        gain_total[0],
        gain_total[1],
        gain_total[2],
        gain_total[3],
    )


def solution(mesh):
    in_specs = (
        P(None, "wide", None),
        P(None, "wide", None),
        P(),
        P("wide", "narrow"),
        P("wide", "narrow"),
        P("wide", "narrow"),
        P("narrow", "wide"),
        P("wide", "narrow"),
        P("wide", "narrow"),
        P("narrow", "wide"),
        P(),
        P(),
        P(),
        P(),
    )
    out_specs = (
        P(None, "wide", None),
        P(None, "wide", None),
        P("wide", "narrow"),
        P("wide", "narrow"),
        P("wide", "narrow"),
        P("narrow", "wide"),
        P("wide", "narrow"),
        P("wide", "narrow"),
        P("narrow", "wide"),
        P(),
        P(),
        P(),
        P(),
    )
    return jax.shard_map(local, mesh=mesh, in_specs=in_specs, out_specs=out_specs, check_vma=False)
```

profile of v0, /device:TPU:0, one launch (start us, length us, event | category | flops | bytes accessed | tf_op | source)
XLA Modules:
  0.0 1960.0 jit_solution(11782084816646856816)
XLA Ops:
  14.2 21.9 %all-gather.16.cloned.1.call-done = bf16[2048,256]{1,0:T(8,128)(2,1)} async-done(((bf16[256,256]{1,0:T(8,128)(2,1)}), bf16[2048,256]{1,0:T(8,128)(2,1)}) %all-gather.16.cloned.1.call-update) | async-done | bytes 1048592 | tf_op jit(solution)/shard_map/all_gather | solution.py:249
  39.5 21.8 %all-gather.20.cloned.1.call-done = bf16[2048,256]{1,0:T(8,128)(2,1)} async-done(((bf16[256,256]{1,0:T(8,128)(2,1)}), bf16[2048,256]{1,0:T(8,128)(2,1)}) %all-gather.20.cloned.1.call-update) | async-done | bytes 1048592 | tf_op jit(solution)/shard_map/all_gather | solution.py:248
  72.1 18.9 all-gather.24.cloned.1.call-done
  94.9 21.8 %all-gather.38.cloned.1.call-done = bf16[2048,256]{1,0:T(8,128)(2,1)} async-done(((bf16[256,256]{1,0:T(8,128)(2,1)}), bf16[2048,256]{1,0:T(8,128)(2,1)}) %all-gather.38.cloned.1.call-update) | async-done | bytes 1048592 | tf_op jit(solution)/shard_map/all_gather | solution.py:97
  122.2 20.3 %all-gather.40.cloned.1.call-done = bf16[2048,256]{0,1:T(8,128)(2,1)} async-done(((bf16[256,256]{0,1:T(8,128)(2,1)}), bf16[2048,256]{0,1:T(8,128)(2,1)}) %all-gather.40.cloned.1.call-update) | async-done | bytes 1048592 | tf_op jit(solution)/shard_map/all_gather | solution.py:96
  150.4 22.0 %all-gather.26.cloned.1.call-done = bf16[512,2048]{1,0:T(8,128)(2,1)} async-done(((bf16[512,256]{1,0:T(8,128)(2,1)}), bf16[512,2048]{1,0:T(8,128)(2,1)}) %all-gather.26.cloned.1.call-update) | async-done | bytes 2097168 | tf_op jit(solution)/shard_map/all_gather | solution.py:250
  175.8 52.0 %all-reduce.25.cloned.1.call-done = bf16[256,2048]{1,0:T(8,128)(2,1)} async-done(((bf16[256,2048]{1,0:T(8,128)(2,1)}), bf16[256,2048]{1,0:T(8,128)(2,1)}) %all-reduce.25.cloned.1.call-update) | async-done | bytes 1048592 | tf_op jit(solution)/shard_map/psum | solution.py:110
  262.1 20.4 %all-gather.18.cloned.1.call-done = bf16[2048,256]{1,0:T(8,128)(2,1)} async-done(((bf16[256,256]{1,0:T(8,128)(2,1)}), bf16[2048,256]{1,0:T(8,128)(2,1)}) %all-gather.18.cloned.1.call-update) | async-done | bytes 1048592 | tf_op jit(solution)/shard_map/all_gather | solution.py:97
  284.6 23.5 %all-gather.34.cloned.1.call-done = bf16[2048,256]{1,0:T(8,128)(2,1)} async-done(((bf16[256,256]{1,0:T(8,128)(2,1)}), bf16[2048,256]{1,0:T(8,128)(2,1)}) %all-gather.34.cloned.1.call-update) | async-done | bytes 1048592 | tf_op jit(solution)/shard_map/all_gather | solution.py:97
  310.5 23.6 %all-gather.44.cloned.1.call-done = bf16[2048,256]{0,1:T(8,128)(2,1)} async-done(((bf16[256,256]{0,1:T(8,128)(2,1)}), bf16[2048,256]{0,1:T(8,128)(2,1)}) %all-gather.44.cloned.1.call-update) | async-done | bytes 1048592 | tf_op jit(solution)/shard_map/all_gather | solution.py:96
  344.3 15.1 all-gather.22.cloned.1.call-done
  369.8 15.0 all-gather.36.cloned.1.call-done
  395.0 36.9 %all-gather.28.cloned.1.call-done = bf16[2048,1536]{1,0:T(8,128)(2,1)} async-done(((bf16[256,1536]{1,0:T(8,128)(2,1)}), bf16[2048,1536]{1,0:T(8,128)(2,1)}) %all-gather.28.cloned.1.call-update) | async-done | bytes 6291472 | tf_op jit(solution)/shard_map/all_gather | solution.py:251
  437.6 42.6 %all-gather.32.cloned.1.call-done = bf16[1536,2048]{1,0:T(8,128)(2,1)} async-done(((bf16[1536,256]{1,0:T(8,128)(2,1)}), bf16[1536,2048]{1,0:T(8,128)(2,1)}) %all-gather.32.cloned.1.call-update) | async-done | bytes 6291472 | tf_op jit(solution)/shard_map/all_gather | solution.py:253
  486.3 41.1 %all-gather.30.cloned.1.call-done = bf16[2048,1536]{1,0:T(8,128)(2,1)} async-done(((bf16[256,1536]{1,0:T(8,128)(2,1)}), bf16[2048,1536]{1,0:T(8,128)(2,1)}) %all-gather.30.cloned.1.call-update) | async-done | bytes 6291472 | tf_op jit(solution)/shard_map/all_gather | solution.py:252
  527.4 6.8 multiply_convert_fusion.9
  543.0 155.1 %all-reduce.31.cloned.1.call-done = (bf16[256,2048]{1,0:T(8,128)(2,1)}, bf16[256,2048]{1,0:T(8,128)(2,1)}, bf16[256,2048]{1,0:T(8,128)(2,1)}, bf16[256,2048]{1,0:T(8,128)(2,1)}) async-done(((bf16[256,2048]{1,0:T(8,128)(2,1)}, bf16[256,2048]{1,0:T(8,128)(2,1)}, bf16[256,2048]{1,0:T(8,128)(2,1)}, bf16[256,2048]{1,0:T(8,128)(2,1)}), (bf16[256,2048]{1,0:T(8,128)(2,1)}, bf16[256,2048]{1,0:T(8,128)(2,1)}, ...) | async-done | bytes 4194320 | tf_op jit(solution)/shard_map/psum | solution.py:110
  706.5 6.9 fusion.382
  770.9 119.5 %all-reduce.29.cloned.1.call-done = (bf16[256,2048]{1,0:T(8,128)(2,1)}, bf16[256,2048]{1,0:T(8,128)(2,1)}, bf16[256,2048]{1,0:T(8,128)(2,1)}) async-done(((bf16[256,2048]{1,0:T(8,128)(2,1)}, bf16[256,2048]{1,0:T(8,128)(2,1)}, bf16[256,2048]{1,0:T(8,128)(2,1)}), (bf16[256,2048]{1,0:T(8,128)(2,1)}, bf16[256,2048]{1,0:T(8,128)(2,1)}, bf16[256,2048]{1,0:T(8,128)(2,1)})) %all-reduce.29.cloned.1.call-update) | async-done | bytes 3145744 | tf_op jit(solution)/shard_map/psum | solution.py:137
  890.4 7.6 multiply_reduce_fusion
  925.0 6.6 fusion.9
  932.6 6.7 fusion.11
  942.0 6.6 fusion
  949.6 6.8 fusion.2
  1026.8 7.6 fusion.398
  1034.4 6.5 fusion.396
  1058.6 15.3 reduce-scatter.20.cloned.1.call-done
  1084.1 7.5 fusion.397
  1091.6 22.0 %reduce-scatter.18.cloned.1.call-done = bf16[256,256]{0,1:T(8,128)(2,1)} async-done(((bf16[2048,256]{0,1:T(8,128)(2,1)}), bf16[256,256]{0,1:T(8,128)(2,1)}) %reduce-scatter.18.cloned.1.call-update) | async-done | bytes 131088 | tf_op jit(solution)/shard_map/reduce_scatter | solution.py:168
  1116.7 35.9 %reduce-scatter.22.cloned.1.call-done = bf16[256,256]{0,1:T(8,128)(2,1)} async-done(((bf16[2048,256]{0,1:T(8,128)(2,1)}), bf16[256,256]{0,1:T(8,128)(2,1)}) %reduce-scatter.22.cloned.1.call-update) | async-done | bytes 131088 | tf_op jit(solution)/shard_map/reduce_scatter | solution.py:168
  1156.5 35.3 %reduce-scatter.26.cloned.1.call-done = bf16[256,256]{0,1:T(8,128)(2,1)} async-done(((bf16[2048,256]{0,1:T(8,128)(2,1)}), bf16[256,256]{0,1:T(8,128)(2,1)}) %reduce-scatter.26.cloned.1.call-update) | async-done | bytes 131088 | tf_op jit(solution)/shard_map/reduce_scatter | solution.py:168
  1195.7 35.7 %reduce-scatter.30.cloned.1.call-done = bf16[256,256]{0,1:T(8,128)(2,1)} async-done(((bf16[2048,256]{0,1:T(8,128)(2,1)}), bf16[256,256]{0,1:T(8,128)(2,1)}) %reduce-scatter.30.cloned.1.call-update) | async-done | bytes 131088 | tf_op jit(solution)/shard_map/reduce_scatter | solution.py:168
  1235.1 18.2 add_convert_fusion.2
  1253.5 8.0 fusion.401
  1261.5 6.5 fusion.399
  1268.0 6.4 fusion.400
  1274.4 17.4 add_convert_fusion.1
  1292.9 7.8 fusion.177
  1300.7 6.5 fusion.185
  1307.2 6.3 fusion.181
  1313.5 17.3 add_convert_fusion
  1372.4 27.0 %reduce-scatter.36.cloned.1.call-done = bf16[256,256]{1,0:T(8,128)(2,1)} async-done(((bf16[2048,256]{1,0:T(8,128)(2,1)}), bf16[256,256]{1,0:T(8,128)(2,1)}) %reduce-scatter.36.cloned.1.call-update) | async-done | bytes 131088 | tf_op jit(solution)/shard_map/reduce_scatter | solution.py:269
  1401.1 64.1 %reduce-scatter.40.cloned.1.call-done = bf16[256,1536]{1,0:T(8,128)(2,1)} async-done(((bf16[2048,1536]{1,0:T(8,128)(2,1)}), bf16[256,1536]{1,0:T(8,128)(2,1)}) %reduce-scatter.40.cloned.1.call-update) | async-done | bytes 786448 | tf_op jit(solution)/shard_map/reduce_scatter | solution.py:275
  1467.7 62.7 %reduce-scatter.42.cloned.1.call-done = bf16[256,1536]{1,0:T(8,128)(2,1)} async-done(((bf16[2048,1536]{1,0:T(8,128)(2,1)}), bf16[256,1536]{1,0:T(8,128)(2,1)}) %reduce-scatter.42.cloned.1.call-update) | async-done | bytes 786448 | tf_op jit(solution)/shard_map/reduce_scatter | solution.py:278
  1532.9 62.4 %reduce-scatter.44.cloned.1.call-done = bf16[1536,256]{1,0:T(8,128)(2,1)} async-done(((bf16[1536,2048]{1,0:T(8,128)(2,1)}), bf16[1536,256]{1,0:T(8,128)(2,1)}) %reduce-scatter.44.cloned.1.call-update) | async-done | bytes 786448 | tf_op jit(solution)/shard_map/reduce_scatter | solution.py:281
  1597.7 292.1 %all-reduce.27.cloned.1.call-done = (bf16[256,2048]{1,0:T(8,128)(2,1)}, bf16[256,2048]{1,0:T(8,128)(2,1)}, bf16[256,2048]{1,0:T(8,128)(2,1)}, bf16[256,2048]{1,0...) async-done(((bf16[256,2048]{1,0:T(8,128)(2,1)}, bf16[256,2048]{1,0:T(8,128)(2,1)}, ...) | async-done | bytes 8388624 | tf_op jit(solution)/shard_map/psum | solution.py:122
  1889.9 6.5 fusion.111
  1913.2 39.5 %all-reduce.16 = (f32[2048]{0:T(1024)}, f32[2048]{0:T(1024)}, f32[128]{0:T(128)}, f32[128]{0:T(128)}) all-reduce(f32[2048]{0:T(1024)S(1)} %add_add_fusion.17, f32[2048]{0:T(1024)S(1)} %add_add_fusion.16, f32[128]{0:T(128)S(1)} %add_add_fusion.19, f32[128]{0:T(128)S(1)} %add_add_fusion.18), channel_id=1, replica_groups=mesh['wide'=8,'narrow'=4] {'wide','narrow'}, use_global_device_ids=true, to_apply=%region_91.92 | all-reduce | flops 4352 | bytes 34816 | tf_op jit(solution)/shard_map/psum | solution.py:285
  (850 shorter events, 407.8 us)
Async XLA Ops:
  7.2 28.8 %all-gather.16.cloned.1.call-start = ((), (), s32[]{:S(2)}) async-start(), calls=%async_computation.15 | async-start | bytes 1179648 | tf_op jit(solution)/shard_map/all_gather | solution.py:249
  7.9 53.4 %all-gather.20.cloned.1.call-start = ((), (), s32[]{:S(2)}) async-start(), calls=%async_computation.17 | async-start | bytes 1179648 | tf_op jit(solution)/shard_map/all_gather | solution.py:248
  8.7 82.3 %all-gather.24.cloned.1.call-start = ((), (), s32[]{:S(2)}) async-start(), calls=%async_computation.19 | async-start | bytes 2359296 | tf_op jit(solution)/shard_map/all_gather | solution.py:247
  9.4 107.3 %all-gather.38.cloned.1.call-start = ((), (), s32[]{:S(2)}) async-start(), calls=%async_computation.26 | async-start | bytes 1179648 | tf_op jit(solution)/shard_map/all_gather | solution.py:97
  14.1 24.8 %copy-start.229 = (f32[256]{0:T(256)}, f32[256]{0:T(256)S(1)}, u32[]{:S(2)}) copy-start(f32[256]{0:T(256)S(1)} %fusion.118) | copy-start | bytes 3076
  14.1 103.9 %copy-start.194 = (f32[256]{0:T(256)}, f32[256]{0:T(256)S(1)}, u32[]{:S(2)}) copy-start(f32[256]{0:T(256)S(1)} %fusion.321) | copy-start | bytes 3076
  38.7 103.8 %all-gather.40.cloned.1.call-start = ((), (), s32[]{:S(2)}) async-start(), calls=%async_computation.27 | async-start | bytes 1179648 | tf_op jit(solution)/shard_map/all_gather | solution.py:96
  39.5 81.9 %copy-start.56 = (f32[256,128]{0,1:T(8,128)}, f32[256,128]{0,1:T(8,128)S(1)}, u32[]{:S(2)}) copy-start(f32[256,128]{0,1:T(8,128)S(1)} %get-tuple-element.143) | copy-start | bytes 393220
  39.5 81.9 %copy-start.96 = (f32[256,128]{0,1:T(8,128)}, f32[256,128]{0,1:T(8,128)S(1)}, u32[]{:S(2)}) copy-start(f32[256,128]{0,1:T(8,128)S(1)} %get-tuple-element.144) | copy-start | bytes 393220
  66.5 105.9 %all-gather.26.cloned.1.call-start = ((), (), s32[]{:S(2)}) async-start(), calls=%async_computation.20 | async-start | bytes 2359296 | tf_op jit(solution)/shard_map/all_gather | solution.py:250
  67.1 160.7 %all-reduce.25.cloned.1.call-start = ((), (), s32[]{:S(2)}) async-start(), calls=%async_computation.28 | async-start | bytes 2097152 | tf_op jit(solution)/shard_map/psum | solution.py:110
  118.1 28.4 %copy-start.81 = (bf16[2048,2,128]{2,1,0:T(2,128)(2,1)}, bf16[2048,2,128]{2,1,0:T(2,128)(2,1)S(1)}, u32[]{:S(2)}) copy-start(bf16[2048,2,128]{2,1,0:T(2,128)(2,1)S(1)} %reshape.1307) | copy-start | bytes 3145732
  150.3 25.3 %copy-start.156 = (bf16[2,128,2,256]{3,1,2,0:T(8,128)(2,1)}, bf16[2,128,2,256]{3,1,2,0:T(8,128)(2,1)S(1)}, u32[]{:S(2)}) copy-start(bf16[2,128,2,256]{3,1,2,0:T(8,128)(2,1)S(1)} %fusion.167) | copy-start | bytes 786436
  175.7 55.6 %copy-start.40 = (bf16[2048,256]{1,0:T(8,128)(2,1)S(1)}, bf16[2048,256]{1,0:T(8,128)(2,1)}, u32[]{:S(2)}) copy-start(bf16[2048,256]{1,0:T(8,128)(2,1)} %all-gather.16.cloned.1.call-done) | copy-start | bytes 3145732
  175.7 83.8 %all-gather.42.cloned.1.call-start = ((), (), s32[]{:S(2)}) async-start(), calls=%async_computation.29 | async-start | bytes 1179648 | tf_op jit(solution)/shard_map/all_gather | solution.py:97
  233.7 48.7 %all-gather.18.cloned.1.call-start = ((), (), s32[]{:S(2)}) async-start(), calls=%async_computation.16 | async-start | bytes 1179648 | tf_op jit(solution)/shard_map/all_gather | solution.py:97
  236.4 71.8 %all-gather.34.cloned.1.call-start = ((), (), s32[]{:S(2)}) async-start(), calls=%async_computation.24 | async-start | bytes 1179648 | tf_op jit(solution)/shard_map/all_gather | solution.py:97
  241.7 92.4 %all-gather.44.cloned.1.call-start = ((), (), s32[]{:S(2)}) async-start(), calls=%async_computation.30 | async-start | bytes 1179648 | tf_op jit(solution)/shard_map/all_gather | solution.py:96
  246.5 112.8 %all-gather.22.cloned.1.call-start = ((), (), s32[]{:S(2)}) async-start(), calls=%async_computation.18 | async-start | bytes 1179648 | tf_op jit(solution)/shard_map/all_gather | solution.py:96
  247.9 136.9 %all-gather.36.cloned.1.call-start = ((), (), s32[]{:S(2)}) async-start(), calls=%async_computation.25 | async-start | bytes 1179648 | tf_op jit(solution)/shard_map/all_gather | solution.py:96
  249.2 182.8 %all-gather.28.cloned.1.call-start = ((), (), s32[]{:S(2)}) async-start(), calls=%async_computation.21 | async-start | bytes 7077888 | tf_op jit(solution)/shard_map/all_gather | solution.py:251
  249.7 230.5 %all-gather.32.cloned.1.call-start = ((), (), s32[]{:S(2)}) async-start(), calls=%async_computation.23 | async-start | bytes 7077888 | tf_op jit(solution)/shard_map/all_gather | solution.py:253
  250.3 277.1 %all-gather.30.cloned.1.call-start = ((), (), s32[]{:S(2)}) async-start(), calls=%async_computation.22 | async-start | bytes 7077888 | tf_op jit(solution)/shard_map/all_gather | solution.py:252
  250.9 447.3 %all-reduce.31.cloned.1.call-start = ((), (), s32[]{:S(2)}) async-start(), calls=%async_computation.48 | async-start | bytes 8388608 | tf_op jit(solution)/shard_map/psum | solution.py:110
  257.7 76.5 %copy-start.136 = (bf16[256,4,128]{0,2,1:T(8,128)(2,1)}, bf16[256,4,128]{0,2,1:T(8,128)(2,1)S(1)}, u32[]{:S(2)}) copy-start(bf16[256,4,128]{0,2,1:T(8,128)(2,1)S(1)} %fusion.248) | copy-start | bytes 786436
  259.0 125.8 %copy-start.134 = (bf16[256,4,128]{0,2,1:T(8,128)(2,1)}, bf16[256,4,128]{0,2,1:T(8,128)(2,1)S(1)}, u32[]{:S(2)}) copy-start(bf16[256,4,128]{0,2,1:T(8,128)(2,1)S(1)} %fusion.244) | copy-start | bytes 786436
  259.5 267.9 %copy-start.50 = (bf16[256,2048]{1,0:T(8,128)(2,1)}, bf16[256,2048]{1,0:T(8,128)(2,1)S(1)}, u32[]{:S(2)}) copy-start(bf16[256,2048]{1,0:T(8,128)(2,1)S(1)} %multiply_convert_fusion.1) | copy-start | bytes 3145732
  543.0 347.4 %all-reduce.29.cloned.1.call-start = ((), (), s32[]{:S(2)}) async-start(), calls=%async_computation.47 | async-start | bytes 6291456 | tf_op jit(solution)/shard_map/psum | solution.py:137
  733.0 26.6 %copy-start.110 = (bf16[256,1536]{1,0:T(8,128)(2,1)}, bf16[256,1536]{1,0:T(8,128)(2,1)S(1)}, u32[]{:S(2)}) copy-start(bf16[256,1536]{1,0:T(8,128)(2,1)S(1)} %get-tuple-element.99) | copy-start | bytes 2359300
  770.1 278.1 %reduce-scatter.24.cloned.1.call-start = ((), (), s32[]{:S(2)}) async-start(), calls=%async_computation.35 | async-start | bytes 1179648 | tf_op jit(solution)/shard_map/reduce_scatter | solution.py:162
  770.8 144.9 %copy-start.190 = (f32[2,2,256]{2,1,0:T(2,128)}, f32[2,2,256]{2,1,0:T(2,128)S(1)}, u32[]{:S(2)}) copy-start(f32[2,2,256]{2,1,0:T(2,128)S(1)} %log_add_fusion.1) | copy-start | bytes 12292
  770.8 178.7 %copy-start.188 = (f32[2,2,256]{2,1,0:T(2,128)}, f32[2,2,256]{2,1,0:T(2,128)S(1)}, u32[]{:S(2)}) copy-start(f32[2,2,256]{2,1,0:T(2,128)S(1)} %log_add_fusion) | copy-start | bytes 12292
  920.7 129.1 %reduce-scatter.16.cloned.1.call-start = ((), (), s32[]{:S(2)}) async-start(), calls=%async_computation.31 | async-start | bytes 1179648 | tf_op jit(solution)/shard_map/reduce_scatter | solution.py:162
  941.9 109.7 %reduce-scatter.28.cloned.1.call-start = ((), (), s32[]{:S(2)}) async-start(), calls=%async_computation.37 | async-start | bytes 1179648 | tf_op jit(solution)/shard_map/reduce_scatter | solution.py:162
  958.9 114.9 %reduce-scatter.20.cloned.1.call-start = ((), (), s32[]{:S(2)}) async-start(), calls=%async_computation.33 | async-start | bytes 1179648 | tf_op jit(solution)/shard_map/reduce_scatter | solution.py:162
  969.1 144.5 %reduce-scatter.18.cloned.1.call-start = ((), (), s32[]{:S(2)}) async-start(), calls=%async_computation.32 | async-start | bytes 1179648 | tf_op jit(solution)/shard_map/reduce_scatter | solution.py:168
  980.4 172.2 %reduce-scatter.22.cloned.1.call-start = ((), (), s32[]{:S(2)}) async-start(), calls=%async_computation.34 | async-start | bytes 1179648 | tf_op jit(solution)/shard_map/reduce_scatter | solution.py:168
  991.2 200.6 %reduce-scatter.26.cloned.1.call-start = ((), (), s32[]{:S(2)}) async-start(), calls=%async_computation.36 | async-start | bytes 1179648 | tf_op jit(solution)/shard_map/reduce_scatter | solution.py:168
  1003.1 228.3 %reduce-scatter.30.cloned.1.call-start = ((), (), s32[]{:S(2)}) async-start(), calls=%async_computation.38 | async-start | bytes 1179648 | tf_op jit(solution)/shard_map/reduce_scatter | solution.py:168
  1017.1 349.9 %reduce-scatter.32.cloned.1.call-start = ((), (), s32[]{:S(2)}) async-start(), calls=%async_computation.39 | async-start | bytes 2359296 | tf_op jit(solution)/shard_map/reduce_scatter | solution.py:263
  1025.6 343.1 %reduce-scatter.38.cloned.1.call-start = ((), (), s32[]{:S(2)}) async-start(), calls=%async_computation.42 | async-start | bytes 2359296 | tf_op jit(solution)/shard_map/reduce_scatter | solution.py:272
  1048.1 322.7 %reduce-scatter.34.cloned.1.call-start = ((), (), s32[]{:S(2)}) async-start(), calls=%async_computation.40 | async-start | bytes 1179648 | tf_op jit(solution)/shard_map/reduce_scatter | solution.py:266
  1083.6 315.9 %reduce-scatter.36.cloned.1.call-start = ((), (), s32[]{:S(2)}) async-start(), calls=%async_computation.41 | async-start | bytes 1179648 | tf_op jit(solution)/shard_map/reduce_scatter | solution.py:269
  1235.0 230.2 %reduce-scatter.40.cloned.1.call-start = ((), (), s32[]{:S(2)}) async-start(), calls=%async_computation.43 | async-start | bytes 7077888 | tf_op jit(solution)/shard_map/reduce_scatter | solution.py:275
  1253.3 277.1 %reduce-scatter.42.cloned.1.call-start = ((), (), s32[]{:S(2)}) async-start(), calls=%async_computation.44 | async-start | bytes 7077888 | tf_op jit(solution)/shard_map/reduce_scatter | solution.py:278
  1291.8 303.5 %reduce-scatter.44.cloned.1.call-start = ((), (), s32[]{:S(2)}) async-start(), calls=%async_computation.45 | async-start | bytes 7077888 | tf_op jit(solution)/shard_map/reduce_scatter | solution.py:281
  1330.8 559.0 %all-reduce.27.cloned.1.call-start = ((), (), s32[]{:S(2)}) async-start(), calls=%async_computation.46 | async-start | bytes 16777216 | tf_op jit(solution)/shard_map/psum | solution.py:122
  1467.7 422.1 %copy-start.202 = (f32[256]{0:T(256)S(1)}, f32[256]{0:T(256)}, u32[]{:S(2)}) copy-start(f32[256]{0:T(256)} %copy-done.199) | copy-start | bytes 3076
  (251 other events, 1176.5 us)
Sparse Core Ops, SparseCore 0:
  9.9 26.0 all-gather.15
  37.9 23.3 all-gather.19
  63.2 27.7 all-gather.23
  93.3 23.3 all-gather.37
  119.0 23.4 all-gather.39
  144.3 28.0 all-gather.25
  175.8 51.8 all-reduce.24
  233.9 22.6 all-gather.41
  259.0 23.3 all-gather.17
  284.8 23.3 all-gather.33
  310.6 23.4 all-gather.43
  335.9 23.4 all-gather.21
  361.2 23.4 all-gather.35
  386.5 45.3 all-gather.27
  433.6 46.5 all-gather.31
  482.0 45.3 all-gather.29
  543.1 155.0 all-reduce.30
  770.3 120.0 all-reduce.28
  920.9 34.9 reduce-scatter.23
  959.5 35.9 reduce-scatter.15
  998.7 35.9 reduce-scatter.27
  1037.8 35.9 reduce-scatter.19
  1077.6 35.9 reduce-scatter.17
  1116.6 35.9 reduce-scatter.21
  1155.8 35.9 reduce-scatter.25
  1195.4 35.9 reduce-scatter.29
  1234.5 41.1 reduce-scatter.31
  1279.0 41.1 reduce-scatter.37
  1323.9 35.9 reduce-scatter.33
  1363.5 35.9 reduce-scatter.35
  1403.4 61.7 reduce-scatter.39
  1468.6 61.7 reduce-scatter.41
  1533.7 61.5 reduce-scatter.43
  1598.7 291.0 all-reduce.26
where the time goes:
time: 1970 us; the launch traced here: 1960 us
  waiting for transfers between devices  1330 us (68%)
  matrix products  388 us (20%)
  other arithmetic  128 us (6%)
  local copies, waits for them, and re-layouts  54.3 us (3%)
  blocking collectives  39.5 us (2%)
    psum x1, waiting for transfers between devices, one_batch(): lax.psum(ffn_part.astype(jnp.bfloat16), 'narrow').astype(jnp.float32)  292 us
    psum x2, waiting for transfers between devices, one_batch(): lax.psum(attn_part.astype(jnp.bfloat16), 'narrow').astype(jnp.float32)  207 us
    reduce_scatter x4, waiting for transfers between devices, one_batch(): lax.psum_scatter(grad_valueall.reshape(total, groups * HD).astype(jnp.bfl...  129 us
    psum x1, waiting for transfers between devices, one_batch(): lax.psum(partial_two.astype(jnp.bfloat16), 'narrow').astype(jnp.float32)  119 us
    all_gather x4, waiting for transfers between devices, one_batch(): lax.all_gather(key_low, 'wide', axis=0, tiled=True)  74 us
    all_gather x4, waiting for transfers between devices, one_batch(): lax.all_gather(value_low, 'wide', axis=0, tiled=True)  65.8 us
    reduce_scatter x1, waiting for transfers between devices, local(): lax.psum_scatter(totals[4].astype(jnp.bfloat16), 'wide', scatter_dimensio...  64.1 us
    reduce_scatter x1, waiting for transfers between devices, local(): lax.psum_scatter(totals[5].astype(jnp.bfloat16), 'wide', scatter_dimensio...  62.7 us
  transfers between devices with their start and end apart: 34, of which 28 were waited for; matrix products, arithmetic and copies ran while one was open for 20% of the time, Pallas kernels for 0%

commit v1 on v0

--- a/solution.py
+++ b/solution.py
@@ -134,7 +134,11 @@
     gain_two = jnp.sum(partial_two * unit_two, axis=0)
     grad_middle = (
         grad_float
-        + pull_two(lax.psum(partial_two.astype(jnp.bfloat16), "narrow").astype(jnp.float32))[0]
+        + pull_two(
+            jnp.sum(lax.all_gather(partial_two.astype(jnp.bfloat16), "narrow"), axis=0).astype(
+                jnp.float32
+            )
+        )[0]
     )
     middle_low = grad_middle.astype(jnp.bfloat16)
     grad_wout = jnp.einsum("th,td->hd", mixed_low, middle_low, preferred_element_type=jnp.float32)

time: 1970 us -> 2080 us (1.056)
  waiting for transfers between devices: 1330 us -> 1430 us
  other arithmetic: 128 us -> 150 us
    all_gather x0 -> x4, waiting for transfers between devices: none -> 263 us  [one_batch(): lax.all_gather(partial_two.astype(jnp.bfloat16), 'narrow')]
    psum x1 -> x0, waiting for transfers between devices: 119 us -> none  [one_batch(): lax.psum(partial_two.astype(jnp.bfloat16), 'narrow').astype(jnp.float32)]
    all_gather x4, waiting for transfers between devices: 74 us -> 36.7 us  [one_batch(): lax.all_gather(key_low, 'wide', axis=0, tiled=True)]
    psum x2, waiting for transfers between devices: 207 us -> 170 us  [one_batch(): lax.psum(attn_part.astype(jnp.bfloat16), 'narrow').astype(jnp.float32)]
    reduce_scatter x1, waiting for transfers between devices: 27 us -> 0.01 us  [local(): lax.psum_scatter(totals[2].astype(jnp.bfloat16), 'wide', scatter_dimensio...]
    reduce_scatter x4, waiting for transfers between devices: 15.3 us -> 36.9 us  [one_batch(): lax.psum_scatter(grad_keyall.reshape(total, groups * HD).astype(jnp.bfloa...]
  transfers between devices with their start and end apart: 34 -> 37, of which waited for: 28 -> 30; matrix products, arithmetic and copies ran while one was open for 20% -> 22% of each run, Pallas kernels for 0% -> 0%
where the time goes in v1:
time: 2080 us; the launch traced here: 2070 us
  waiting for transfers between devices  1430 us (69%)
  matrix products  382 us (18%)
  other arithmetic  150 us (7%)
  local copies, waits for them, and re-layouts  51.4 us (2%)
  blocking collectives  39.5 us (2%)
    psum x1, waiting for transfers between devices, one_batch(): lax.psum(ffn_part.astype(jnp.bfloat16), 'narrow').astype(jnp.float32)  292 us
    all_gather x4, waiting for transfers between devices, one_batch(): lax.all_gather(partial_two.astype(jnp.bfloat16), 'narrow')  263 us
    psum x2, waiting for transfers between devices, one_batch(): lax.psum(attn_part.astype(jnp.bfloat16), 'narrow').astype(jnp.float32)  170 us
    reduce_scatter x4, waiting for transfers between devices, one_batch(): lax.psum_scatter(grad_valueall.reshape(total, groups * HD).astype(jnp.bfl...  142 us
    all_gather x4, waiting for transfers between devices, one_batch(): lax.all_gather(value_low, 'wide', axis=0, tiled=True)  81.5 us
    reduce_scatter x1, waiting for transfers between devices, local(): lax.psum_scatter(totals[5].astype(jnp.bfloat16), 'wide', scatter_dimensio...  62.7 us
    reduce_scatter x1, waiting for transfers between devices, local(): lax.psum_scatter(totals[6].astype(jnp.bfloat16), 'wide', scatter_dimensio...  62.4 us
    reduce_scatter x1, waiting for transfers between devices, local(): lax.psum_scatter(totals[4].astype(jnp.bfloat16), 'wide', scatter_dimensio...  62.4 us
  transfers between devices with their start and end apart: 37, of which 30 were waited for; matrix products, arithmetic and copies ran while one was open for 22% of the time, Pallas kernels for 0%

profile of v1, /device:TPU:0, one launch (start us, length us, event | category | flops | bytes accessed | tf_op | source)
XLA Modules:
  0.0 2072.7 jit_solution(1971729719539140949)
XLA Ops:
  14.1 21.9 %all-gather.24.cloned.1.call-done = bf16[2048,256]{1,0:T(8,128)(2,1)} async-done(((bf16[256,256]{1,0:T(8,128)(2,1)}), bf16[2048,256]{1,0:T(8,128)(2,1)}) %all-gather.24.cloned.1.call-update) | async-done | bytes 1048592 | tf_op jit(solution)/shard_map/all_gather | solution.py:253
  40.2 21.1 %all-gather.28.cloned.1.call-done = bf16[2048,256]{1,0:T(8,128)(2,1)} async-done(((bf16[256,256]{1,0:T(8,128)(2,1)}), bf16[2048,256]{1,0:T(8,128)(2,1)}) %all-gather.28.cloned.1.call-update) | async-done | bytes 1048592 | tf_op jit(solution)/shard_map/all_gather | solution.py:252
  71.8 19.2 all-gather.32.cloned.1.call-done
  94.9 21.8 %all-gather.46.cloned.1.call-done = bf16[2048,256]{1,0:T(8,128)(2,1)} async-done(((bf16[256,256]{1,0:T(8,128)(2,1)}), bf16[2048,256]{1,0:T(8,128)(2,1)}) %all-gather.46.cloned.1.call-update) | async-done | bytes 1048592 | tf_op jit(solution)/shard_map/all_gather | solution.py:97
  122.2 20.3 all-gather.48.cloned.1.call-done
  150.3 22.1 %all-gather.34.cloned.1.call-done = bf16[512,2048]{1,0:T(8,128)(2,1)} async-done(((bf16[512,256]{1,0:T(8,128)(2,1)}), bf16[512,2048]{1,0:T(8,128)(2,1)}) %all-gather.34.cloned.1.call-update) | async-done | bytes 2097168 | tf_op jit(solution)/shard_map/all_gather | solution.py:254
  176.5 51.3 %all-reduce.23.cloned.1.call-done = bf16[256,2048]{1,0:T(8,128)(2,1)} async-done(((bf16[256,2048]{1,0:T(8,128)(2,1)}), bf16[256,2048]{1,0:T(8,128)(2,1)}) %all-reduce.23.cloned.1.call-update) | async-done | bytes 1048592 | tf_op jit(solution)/shard_map/psum | solution.py:110
  269.8 13.6 all-gather.50.cloned.1.call-done
  285.5 23.0 %all-gather.26.cloned.1.call-done = bf16[2048,256]{1,0:T(8,128)(2,1)} async-done(((bf16[256,256]{1,0:T(8,128)(2,1)}), bf16[2048,256]{1,0:T(8,128)(2,1)}) %all-gather.26.cloned.1.call-update) | async-done | bytes 1048592 | tf_op jit(solution)/shard_map/all_gather | solution.py:97
  310.7 23.1 %all-gather.42.cloned.1.call-done = bf16[2048,256]{1,0:T(8,128)(2,1)} async-done(((bf16[256,256]{1,0:T(8,128)(2,1)}), bf16[2048,256]{1,0:T(8,128)(2,1)}) %all-gather.42.cloned.1.call-update) | async-done | bytes 1048592 | tf_op jit(solution)/shard_map/all_gather | solution.py:97
  335.9 45.0 %all-gather.36.cloned.1.call-done = bf16[2048,1536]{1,0:T(8,128)(2,1)} async-done(((bf16[256,1536]{1,0:T(8,128)(2,1)}), bf16[2048,1536]{1,0:T(8,128)(2,1)}) %all-gather.36.cloned.1.call-update) | async-done | bytes 6291472 | tf_op jit(solution)/shard_map/all_gather | solution.py:255
  386.7 42.8 %all-gather.40.cloned.1.call-done = bf16[1536,2048]{1,0:T(8,128)(2,1)} async-done(((bf16[1536,256]{1,0:T(8,128)(2,1)}), bf16[1536,2048]{1,0:T(8,128)(2,1)}) %all-gather.40.cloned.1.call-update) | async-done | bytes 6291472 | tf_op jit(solution)/shard_map/all_gather | solution.py:257
  435.5 41.1 %all-gather.38.cloned.1.call-done = bf16[2048,1536]{1,0:T(8,128)(2,1)} async-done(((bf16[256,1536]{1,0:T(8,128)(2,1)}), bf16[2048,1536]{1,0:T(8,128)(2,1)}) %all-gather.38.cloned.1.call-update) | async-done | bytes 6291472 | tf_op jit(solution)/shard_map/all_gather | solution.py:256
  476.6 6.8 multiply_convert_fusion.9
  512.0 15.1 all-gather.44.cloned.1.call-done
  537.6 71.7 %all-gather.58.cloned.1.call-done = bf16[1024,2048]{1,0:T(8,128)(2,1)} async-done(((bf16[256,2048]{1,0:T(8,128)(2,1)}), bf16[1024,2048]{1,0:T(8,128)(2,1)}) %all-gather.58.cloned.1.call-update) | async-done | bytes 4194320 | tf_op jit(solution)/shard_map/all_gather | solution.py:138
  613.6 118.9 %all-reduce.27.cloned.1.call-done = (bf16[256,2048]{1,0:T(8,128)(2,1)}, bf16[256,2048]{1,0:T(8,128)(2,1)}, bf16[256,2048]{1,0:T(8,128)(2,1)}) async-done(((bf16[256,2048]{1,0:T(8,128)(2,1)}, bf16[256,2048]{1,0:T(8,128)(2,1)}, bf16[256,2048]{1,0:T(8,128)(2,1)}), (bf16[256,2048]{1,0:T(8,128)(2,1)}, bf16[256,2048]{1,0:T(8,128)(2,1)}, bf16[256,2048]{1,0:T(8,128)(2,1)})) %all-reduce.27.cloned.1.call-update) | async-done | bytes 3145744 | tf_op jit(solution)/shard_map/psum | solution.py:110
  801.0 38.1 %all-gather.56.cloned.1.call-done = bf16[1024,2048]{1,0:T(8,128)(2,1)} async-done(((bf16[256,2048]{1,0:T(8,128)(2,1)}), bf16[1024,2048]{1,0:T(8,128)(2,1)}) %all-gather.56.cloned.1.call-update) | async-done | bytes 4194320 | tf_op jit(solution)/shard_map/all_gather | solution.py:138
  843.4 76.4 %all-gather.60.cloned.1.call-done = bf16[1024,2048]{1,0:T(8,128)(2,1)} async-done(((bf16[256,2048]{1,0:T(8,128)(2,1)}), bf16[1024,2048]{1,0:T(8,128)(2,1)}) %all-gather.60.cloned.1.call-update) | async-done | bytes 4194320 | tf_op jit(solution)/shard_map/all_gather | solution.py:138
  924.1 76.6 %all-gather.54.cloned.1.call-done = bf16[1024,2048]{1,0:T(8,128)(2,1)} async-done(((bf16[256,2048]{1,0:T(8,128)(2,1)}), bf16[1024,2048]{1,0:T(8,128)(2,1)}) %all-gather.54.cloned.1.call-update) | async-done | bytes 4194320 | tf_op jit(solution)/shard_map/all_gather | solution.py:138
  1004.9 7.1 multiply_reduce_fusion
  1040.1 6.6 fusion.9
  1047.7 6.7 fusion.11
  1057.0 6.5 fusion
  1064.5 6.8 fusion.2
  1151.9 35.4 %reduce-scatter.20.cloned.1.call-done = bf16[256,256]{0,1:T(8,128)(2,1)} async-done(((bf16[2048,256]{0,1:T(8,128)(2,1)}), bf16[256,256]{0,1:T(8,128)(2,1)}) %reduce-scatter.20.cloned.1.call-update) | async-done | bytes 131088 | tf_op jit(solution)/shard_map/reduce_scatter | solution.py:166
  1194.4 32.6 %reduce-scatter.18.cloned.1.call-done = bf16[256,256]{0,1:T(8,128)(2,1)} async-done(((bf16[2048,256]{0,1:T(8,128)(2,1)}), bf16[256,256]{0,1:T(8,128)(2,1)}) %reduce-scatter.18.cloned.1.call-update) | async-done | bytes 131088 | tf_op jit(solution)/shard_map/reduce_scatter | solution.py:172
  1228.8 37.2 %reduce-scatter.22.cloned.1.call-done = bf16[256,256]{0,1:T(8,128)(2,1)} async-done(((bf16[2048,256]{0,1:T(8,128)(2,1)}), bf16[256,256]{0,1:T(8,128)(2,1)}) %reduce-scatter.22.cloned.1.call-update) | async-done | bytes 131088 | tf_op jit(solution)/shard_map/reduce_scatter | solution.py:172
  1269.1 36.0 %reduce-scatter.26.cloned.1.call-done = bf16[256,256]{0,1:T(8,128)(2,1)} async-done(((bf16[2048,256]{0,1:T(8,128)(2,1)}), bf16[256,256]{0,1:T(8,128)(2,1)}) %reduce-scatter.26.cloned.1.call-update) | async-done | bytes 131088 | tf_op jit(solution)/shard_map/reduce_scatter | solution.py:172
  1309.1 35.8 %reduce-scatter.30.cloned.1.call-done = bf16[256,256]{0,1:T(8,128)(2,1)} async-done(((bf16[2048,256]{0,1:T(8,128)(2,1)}), bf16[256,256]{0,1:T(8,128)(2,1)}) %reduce-scatter.30.cloned.1.call-update) | async-done | bytes 131088 | tf_op jit(solution)/shard_map/reduce_scatter | solution.py:172
  1357.5 7.7 fusion.398
  1365.2 6.5 fusion.396
  1371.7 6.3 fusion.397
  1378.1 17.4 add_convert_fusion.2
  1395.7 8.0 fusion.401
  1403.7 6.5 fusion.399
  1410.2 6.3 fusion.400
  1416.5 17.2 add_convert_fusion.1
  1434.8 7.8 fusion.177
  1442.6 6.5 fusion.185
  1449.1 6.3 fusion.181
  1455.4 17.3 add_convert_fusion
  1515.8 62.4 %reduce-scatter.40.cloned.1.call-done = bf16[256,1536]{1,0:T(8,128)(2,1)} async-done(((bf16[2048,1536]{1,0:T(8,128)(2,1)}), bf16[256,1536]{1,0:T(8,128)(2,1)}) %reduce-scatter.40.cloned.1.call-update) | async-done | bytes 786448 | tf_op jit(solution)/shard_map/reduce_scatter | solution.py:279
  1580.6 62.7 %reduce-scatter.42.cloned.1.call-done = bf16[256,1536]{1,0:T(8,128)(2,1)} async-done(((bf16[2048,1536]{1,0:T(8,128)(2,1)}), bf16[256,1536]{1,0:T(8,128)(2,1)}) %reduce-scatter.42.cloned.1.call-update) | async-done | bytes 786448 | tf_op jit(solution)/shard_map/reduce_scatter | solution.py:282
  1645.8 62.4 %reduce-scatter.44.cloned.1.call-done = bf16[1536,256]{1,0:T(8,128)(2,1)} async-done(((bf16[1536,2048]{1,0:T(8,128)(2,1)}), bf16[1536,256]{1,0:T(8,128)(2,1)}) %reduce-scatter.44.cloned.1.call-update) | async-done | bytes 786448 | tf_op jit(solution)/shard_map/reduce_scatter | solution.py:285
  1710.5 292.0 %all-reduce.25.cloned.1.call-done = (bf16[256,2048]{1,0:T(8,128)(2,1)}, bf16[256,2048]{1,0:T(8,128)(2,1)}, bf16[256,2048]{1,0:T(8,128)(2,1)}, bf16[256,2048]{1,0...) async-done(((bf16[256,2048]{1,0:T(8,128)(2,1)}, bf16[256,2048]{1,0:T(8,128)(2,1)}, ...) | async-done | bytes 8388624 | tf_op jit(solution)/shard_map/psum | solution.py:122
  2002.6 6.5 fusion.111
  2025.9 39.5 %all-reduce.16 = (f32[2048]{0:T(1024)}, f32[2048]{0:T(1024)}, f32[128]{0:T(128)}, f32[128]{0:T(128)}) all-reduce(f32[2048]{0:T(1024)S(1)} %add_add_fusion.17, f32[2048]{0:T(1024)S(1)} %add_add_fusion.16, f32[128]{0:T(128)S(1)} %add_add_fusion.19, f32[128]{0:T(128)S(1)} %add_add_fusion.18), channel_id=1, replica_groups=mesh['wide'=8,'narrow'=4] {'wide','narrow'}, use_global_device_ids=true, to_apply=%region_91.92 | all-reduce | flops 4352 | bytes 34816 | tf_op jit(solution)/shard_map/psum | solution.py:289
  (903 shorter events, 434.1 us)
Async XLA Ops:
  7.2 28.8 %all-gather.24.cloned.1.call-start = ((), (), s32[]{:S(2)}) async-start(), calls=%async_computation.15 | async-start | bytes 1179648 | tf_op jit(solution)/shard_map/all_gather | solution.py:253
  7.9 53.4 %all-gather.28.cloned.1.call-start = ((), (), s32[]{:S(2)}) async-start(), calls=%async_computation.17 | async-start | bytes 1179648 | tf_op jit(solution)/shard_map/all_gather | solution.py:252
  8.7 82.3 %all-gather.32.cloned.1.call-start = ((), (), s32[]{:S(2)}) async-start(), calls=%async_computation.19 | async-start | bytes 2359296 | tf_op jit(solution)/shard_map/all_gather | solution.py:251
  9.4 107.3 %all-gather.46.cloned.1.call-start = ((), (), s32[]{:S(2)}) async-start(), calls=%async_computation.26 | async-start | bytes 1179648 | tf_op jit(solution)/shard_map/all_gather | solution.py:97
  14.1 103.9 %copy-start.193 = (f32[256]{0:T(256)}, f32[256]{0:T(256)S(1)}, u32[]{:S(2)}) copy-start(f32[256]{0:T(256)S(1)} %fusion.321) | copy-start | bytes 3076
  38.7 103.8 %all-gather.48.cloned.1.call-start = ((), (), s32[]{:S(2)}) async-start(), calls=%async_computation.27 | async-start | bytes 1179648 | tf_op jit(solution)/shard_map/all_gather | solution.py:96
  40.1 81.3 %copy-start.60 = (f32[256,128]{0,1:T(8,128)}, f32[256,128]{0,1:T(8,128)S(1)}, u32[]{:S(2)}) copy-start(f32[256,128]{0,1:T(8,128)S(1)} %get-tuple-element.139) | copy-start | bytes 393220
  40.2 81.3 %copy-start.95 = (f32[256,128]{0,1:T(8,128)}, f32[256,128]{0,1:T(8,128)S(1)}, u32[]{:S(2)}) copy-start(f32[256,128]{0,1:T(8,128)S(1)} %get-tuple-element.140) | copy-start | bytes 393220
  66.5 105.9 %all-gather.34.cloned.1.call-start = ((), (), s32[]{:S(2)}) async-start(), calls=%async_computation.20 | async-start | bytes 2359296 | tf_op jit(solution)/shard_map/all_gather | solution.py:254
  67.1 160.7 %all-reduce.23.cloned.1.call-start = ((), (), s32[]{:S(2)}) async-start(), calls=%async_computation.28 | async-start | bytes 2097152 | tf_op jit(solution)/shard_map/psum | solution.py:110
  175.8 86.3 %all-gather.52.cloned.1.call-start = ((), (), s32[]{:S(2)}) async-start(), calls=%async_computation.30 | async-start | bytes 1179648 | tf_op jit(solution)/shard_map/all_gather | solution.py:96
  176.5 79.8 %copy-start.62 = (f32[256,128]{0,1:T(8,128)}, f32[256,128]{0,1:T(8,128)S(1)}, u32[]{:S(2)}) copy-start(f32[256,128]{0,1:T(8,128)S(1)} %get-tuple-element.137) | copy-start | bytes 393220
  176.5 79.8 %copy-start.97 = (f32[256,128]{0,1:T(8,128)}, f32[256,128]{0,1:T(8,128)S(1)}, u32[]{:S(2)}) copy-start(f32[256,128]{0,1:T(8,128)S(1)} %get-tuple-element.138) | copy-start | bytes 393220
  176.5 55.0 %copy-start.152 = (bf16[256,2048]{1,0:T(8,128)(2,1)S(1)}, bf16[256,2048]{1,0:T(8,128)(2,1)}, u32[]{:S(2)}) copy-start(bf16[256,2048]{1,0:T(8,128)(2,1)} %copy-done.151) | copy-start | bytes 3145732
  235.2 48.2 %all-gather.50.cloned.1.call-start = ((), (), s32[]{:S(2)}) async-start(), calls=%async_computation.29 | async-start | bytes 1179648 | tf_op jit(solution)/shard_map/all_gather | solution.py:97
  237.6 70.9 %all-gather.26.cloned.1.call-start = ((), (), s32[]{:S(2)}) async-start(), calls=%async_computation.16 | async-start | bytes 1179648 | tf_op jit(solution)/shard_map/all_gather | solution.py:97
  240.1 93.7 %all-gather.42.cloned.1.call-start = ((), (), s32[]{:S(2)}) async-start(), calls=%async_computation.24 | async-start | bytes 1179648 | tf_op jit(solution)/shard_map/all_gather | solution.py:97
  242.6 138.4 %all-gather.36.cloned.1.call-start = ((), (), s32[]{:S(2)}) async-start(), calls=%async_computation.21 | async-start | bytes 7077888 | tf_op jit(solution)/shard_map/all_gather | solution.py:255
  243.2 186.3 %all-gather.40.cloned.1.call-start = ((), (), s32[]{:S(2)}) async-start(), calls=%async_computation.23 | async-start | bytes 7077888 | tf_op jit(solution)/shard_map/all_gather | solution.py:257
  243.9 232.7 %all-gather.38.cloned.1.call-start = ((), (), s32[]{:S(2)}) async-start(), calls=%async_computation.22 | async-start | bytes 7077888 | tf_op jit(solution)/shard_map/all_gather | solution.py:256
  244.5 257.4 %all-gather.30.cloned.1.call-start = ((), (), s32[]{:S(2)}) async-start(), calls=%async_computation.18 | async-start | bytes 1179648 | tf_op jit(solution)/shard_map/all_gather | solution.py:96
  253.3 273.8 %all-gather.44.cloned.1.call-start = ((), (), s32[]{:S(2)}) async-start(), calls=%async_computation.25 | async-start | bytes 1179648 | tf_op jit(solution)/shard_map/all_gather | solution.py:96
  253.4 479.1 %copy-start.222 = (f32[256]{0:T(256)}, f32[256]{0:T(256)S(1)}, u32[]{:S(2)}) copy-start(f32[256]{0:T(256)S(1)} %fusion.322) | copy-start | bytes 3076
  257.9 351.4 %all-gather.58.cloned.1.call-start = ((), (), s32[]{:S(2)}) async-start(), calls=%async_computation.48 | async-start | bytes 5242880 | tf_op jit(solution)/shard_map/all_gather | solution.py:138
  262.0 214.6 %copy-start.50 = (bf16[256,2048]{1,0:T(8,128)(2,1)}, bf16[256,2048]{1,0:T(8,128)(2,1)S(1)}, u32[]{:S(2)}) copy-start(bf16[256,2048]{1,0:T(8,128)(2,1)S(1)} %multiply_convert_fusion.1) | copy-start | bytes 3145732
  492.4 240.1 %all-reduce.27.cloned.1.call-start = ((), (), s32[]{:S(2)}) async-start(), calls=%async_computation.51 | async-start | bytes 6291456 | tf_op jit(solution)/shard_map/psum | solution.py:110
  537.2 302.0 %all-gather.56.cloned.1.call-start = ((), (), s32[]{:S(2)}) async-start(), calls=%async_computation.47 | async-start | bytes 5242880 | tf_op jit(solution)/shard_map/all_gather | solution.py:138
  759.3 160.6 %all-gather.60.cloned.1.call-start = ((), (), s32[]{:S(2)}) async-start(), calls=%async_computation.49 | async-start | bytes 5242880 | tf_op jit(solution)/shard_map/all_gather | solution.py:138
  780.4 220.2 %all-gather.54.cloned.1.call-start = ((), (), s32[]{:S(2)}) async-start(), calls=%async_computation.46 | async-start | bytes 5242880 | tf_op jit(solution)/shard_map/all_gather | solution.py:138
  800.6 344.0 %reduce-scatter.24.cloned.1.call-start = ((), (), s32[]{:S(2)}) async-start(), calls=%async_computation.35 | async-start | bytes 1179648 | tf_op jit(solution)/shard_map/reduce_scatter | solution.py:166
  800.9 229.2 %copy-start.189 = (f32[2,2,256]{2,1,0:T(2,128)}, f32[2,2,256]{2,1,0:T(2,128)S(1)}, u32[]{:S(2)}) copy-start(f32[2,2,256]{2,1,0:T(2,128)S(1)} %log_add_fusion.1) | copy-start | bytes 12292
  801.0 263.5 %copy-start.187 = (f32[2,2,256]{2,1,0:T(2,128)}, f32[2,2,256]{2,1,0:T(2,128)S(1)}, u32[]{:S(2)}) copy-start(f32[2,2,256]{2,1,0:T(2,128)S(1)} %log_add_fusion) | copy-start | bytes 12292
  1035.3 110.4 %reduce-scatter.16.cloned.1.call-start = ((), (), s32[]{:S(2)}) async-start(), calls=%async_computation.31 | async-start | bytes 1179648 | tf_op jit(solution)/shard_map/reduce_scatter | solution.py:166
  1056.9 91.2 %reduce-scatter.28.cloned.1.call-start = ((), (), s32[]{:S(2)}) async-start(), calls=%async_computation.37 | async-start | bytes 1179648 | tf_op jit(solution)/shard_map/reduce_scatter | solution.py:166
  1073.8 113.6 %reduce-scatter.20.cloned.1.call-start = ((), (), s32[]{:S(2)}) async-start(), calls=%async_computation.33 | async-start | bytes 1179648 | tf_op jit(solution)/shard_map/reduce_scatter | solution.py:166
  1084.1 142.9 %reduce-scatter.18.cloned.1.call-start = ((), (), s32[]{:S(2)}) async-start(), calls=%async_computation.32 | async-start | bytes 1179648 | tf_op jit(solution)/shard_map/reduce_scatter | solution.py:172
  1096.1 169.9 %reduce-scatter.22.cloned.1.call-start = ((), (), s32[]{:S(2)}) async-start(), calls=%async_computation.34 | async-start | bytes 1179648 | tf_op jit(solution)/shard_map/reduce_scatter | solution.py:172
  1108.8 196.3 %reduce-scatter.26.cloned.1.call-start = ((), (), s32[]{:S(2)}) async-start(), calls=%async_computation.36 | async-start | bytes 1179648 | tf_op jit(solution)/shard_map/reduce_scatter | solution.py:172
  1121.7 223.3 %reduce-scatter.30.cloned.1.call-start = ((), (), s32[]{:S(2)}) async-start(), calls=%async_computation.38 | async-start | bytes 1179648 | tf_op jit(solution)/shard_map/reduce_scatter | solution.py:172
  1135.8 372.9 %reduce-scatter.32.cloned.1.call-start = ((), (), s32[]{:S(2)}) async-start(), calls=%async_computation.39 | async-start | bytes 2359296 | tf_op jit(solution)/shard_map/reduce_scatter | solution.py:267
  1144.5 365.9 %reduce-scatter.34.cloned.1.call-start = ((), (), s32[]{:S(2)}) async-start(), calls=%async_computation.40 | async-start | bytes 1179648 | tf_op jit(solution)/shard_map/reduce_scatter | solution.py:270
  1194.3 317.8 %reduce-scatter.36.cloned.1.call-start = ((), (), s32[]{:S(2)}) async-start(), calls=%async_computation.41 | async-start | bytes 1179648 | tf_op jit(solution)/shard_map/reduce_scatter | solution.py:273
  1348.5 165.5 %reduce-scatter.38.cloned.1.call-start = ((), (), s32[]{:S(2)}) async-start(), calls=%async_computation.42 | async-start | bytes 2359296 | tf_op jit(solution)/shard_map/reduce_scatter | solution.py:276
  1356.2 221.9 %reduce-scatter.40.cloned.1.call-start = ((), (), s32[]{:S(2)}) async-start(), calls=%async_computation.43 | async-start | bytes 7077888 | tf_op jit(solution)/shard_map/reduce_scatter | solution.py:279
  1395.4 247.9 %reduce-scatter.42.cloned.1.call-start = ((), (), s32[]{:S(2)}) async-start(), calls=%async_computation.44 | async-start | bytes 7077888 | tf_op jit(solution)/shard_map/reduce_scatter | solution.py:282
  1433.7 274.4 %reduce-scatter.44.cloned.1.call-start = ((), (), s32[]{:S(2)}) async-start(), calls=%async_computation.45 | async-start | bytes 7077888 | tf_op jit(solution)/shard_map/reduce_scatter | solution.py:285
  1472.7 529.8 %all-reduce.25.cloned.1.call-start = ((), (), s32[]{:S(2)}) async-start(), calls=%async_computation.50 | async-start | bytes 16777216 | tf_op jit(solution)/shard_map/psum | solution.py:122
  1580.6 421.9 %copy-start.200 = (f32[256]{0:T(256)S(1)}, f32[256]{0:T(256)}, u32[]{:S(2)}) copy-start(f32[256]{0:T(256)} %copy-done.198) | copy-start | bytes 3076
  (271 other events, 1533.3 us)
Sparse Core Ops, SparseCore 0:
  9.9 26.0 all-gather.23
  37.9 23.3 all-gather.27
  63.2 27.7 all-gather.31
  93.3 23.3 all-gather.45
  119.0 23.4 all-gather.47
  144.3 28.0 all-gather.33
  175.9 51.8 all-reduce.22
  235.3 22.7 all-gather.51
  260.0 23.3 all-gather.49
  285.1 23.3 all-gather.25
  310.4 23.3 all-gather.41
  335.5 45.3 all-gather.35
  382.8 46.5 all-gather.39
  431.2 45.3 all-gather.37
  478.3 23.4 all-gather.29
  503.6 23.5 all-gather.43
  528.5 80.7 all-gather.57
  612.9 119.5 all-reduce.26
  759.4 79.7 all-gather.55
  840.6 79.2 all-gather.59
  921.4 79.2 all-gather.53
  1035.5 34.4 reduce-scatter.23
  1073.1 35.9 reduce-scatter.15
  1112.2 35.9 reduce-scatter.27
  1151.3 35.9 reduce-scatter.19
  1191.0 35.9 reduce-scatter.17
  1230.0 35.9 reduce-scatter.21
  1269.2 35.9 reduce-scatter.25
  1308.9 35.9 reduce-scatter.29
  1348.0 41.1 reduce-scatter.31
  1392.4 35.9 reduce-scatter.33
  1432.1 35.9 reduce-scatter.35
  1471.2 41.1 reduce-scatter.37
  1516.4 61.7 reduce-scatter.39
  1581.5 61.7 reduce-scatter.41
  1646.5 61.5 reduce-scatter.43
  1711.4 291.0 all-reduce.24
